TPU v7x, 32 devices: a whole 2x2x4 slice. The times are simulated.
32 devices in a mesh: blk: 16 (over z, y, x), ga: 2 (over core).
Axes of the slice: x: 2, y: 2, z: 4, core: 2. Of those that a mesh axis runs over, the one named last changes fastest.
Arguments:
- pair_elements: bfloat16 [4096, 16384], P('ga', 'blk'), may hold values from -6 to 6
- screening: bfloat16 [4096, 4096], P('ga', 'blk'), may hold values from -0.09375 to 0.09375
- energies: float32 [256], replicated, may hold values from 0.5 to 3
- frequencies: float32 [8], replicated, may hold values from 0.3 to 3
- qp_index: int32 [32], replicated, may hold values from 0 to 255
- occupied: int32 [256], replicated, may hold values 0 or 1
Outputs:
- self_energy: float32 [2, 8, 32, 32], replicated
All inputs are finite; a program needn't handle non-finite values.
Results may differ from a plain program's by a relative error of at most 0.0003.
Values may be sent and summed in bfloat16 or wider, within the bound.
A program may use at most 128 MiB of HBM per device.

v0:
```python
import jax
import jax.numpy as jnp
from jax import lax
from jax.sharding import PartitionSpec as P

STATES = 32
NG = 4096


def band_weights(energies, frequencies, qp_index, occupied, offset, band_count):
    level_count = energies.shape[0]
    position = jnp.arange(level_count, dtype=jnp.int32)
    signed = jnp.where(occupied == 1, -energies, energies)
    onehot = (qp_index[:, None] == position[None, :]).astype(jnp.float32)
    state_level = jnp.sum(onehot * signed[None, :], axis=1)
    band_level = lax.dynamic_slice_in_dim(signed, offset, band_count, 0)
    detuning = state_level[:, None] - band_level[None, :]
    imag_freq = frequencies[:, None, None]
    modulus = detuning[None] ** 2 + imag_freq**2
    return (detuning[None] / modulus, -imag_freq / modulus)


def window_sigma(elements, screened, weight_real, weight_imag, band_count):
    row_count = elements.shape[0]
    local_elems = elements.astype(jnp.float32).reshape(row_count, band_count, 2, STATES)
    image_cols = screened.reshape(row_count, band_count, 2, STATES)
    intersection = jnp.einsum(
        "gnpi,gnqj->npiqj", local_elems, image_cols, precision=lax.Precision.HIGHEST
    )
    intersection_real = intersection[:, 0, :, 0, :] + intersection[:, 1, :, 1, :]
    intersection_imag = intersection[:, 0, :, 1, :] - intersection[:, 1, :, 0, :]
    sigma_real = jnp.einsum(
        "kin,nij->kij", weight_real, intersection_real, precision=lax.Precision.HIGHEST
    ) - jnp.einsum("kin,nij->kij", weight_imag, intersection_imag, precision=lax.Precision.HIGHEST)
    sigma_imag = jnp.einsum(
        "kin,nij->kij", weight_real, intersection_imag, precision=lax.Precision.HIGHEST
    ) + jnp.einsum("kin,nij->kij", weight_imag, intersection_real, precision=lax.Precision.HIGHEST)
    return jnp.stack([sigma_real, sigma_imag]) / NG


def shards(pair_elements, screening, energies, frequencies, qp_index, occupied):
    col_count = pair_elements.shape[1]
    band_count = col_count // (2 * STATES)
    gathered = lax.all_gather(pair_elements, "ga", axis=0, tiled=True)
    screened = jnp.dot(
        lax.all_gather(screening, "blk", axis=1, tiled=True),
        gathered,
        preferred_element_type=jnp.float32,
    )
    band_start = lax.axis_index("blk") * band_count
    weight_real, weight_imag = band_weights(
        energies, frequencies, qp_index, occupied, band_start, band_count
    )
    partial_value = window_sigma(pair_elements, screened, weight_real, weight_imag, band_count)
    return lax.psum(partial_value, ("blk", "ga"))


def solution(mesh):
    placed = (P("ga", "blk"), P("ga", "blk"), P(), P(), P(), P())
    return jax.shard_map(shards, mesh=mesh, in_specs=placed, out_specs=P(), check_vma=False)
```

profile of v0, /device:TPU:0, one launch (start us, length us, event | category | flops | bytes accessed | tf_op | source)
XLA Modules:
  0.0 443.0 jit_solution(11646669424119894896)
XLA Ops:
  6.5 0.0 copy-start.1
  6.5 0.0 copy-start.2
  6.5 0.0 copy-start.3
  6.5 0.0 copy-start.4
  6.5 0.0 all-gather.5.cloned.1.call-start
  6.6 0.7 all-gather.5.cloned.1.call-update
  7.3 0.0 all-gather.3.cloned.1.call-start
  7.3 0.7 all-gather.3.cloned.1.call-update
  8.0 0.0 all-reduce.2.cloned.1.call-start
  8.1 6.6 %copy.19 = bf16[2048,1024]{0,1:T(8,128)(2,1)} copy(bf16[2048,1024]{1,0:T(8,128)(2,1)} %param.6) | data formatting | bytes 8388608 | tf_op args[0]
  14.7 0.0 copy-done.1
  14.7 0.0 copy-done.2
  14.7 0.1 dynamic_slice.3
  14.7 0.0 copy-done.3
  14.8 0.2 select_reduce_fusion
  14.9 0.0 copy-done.4
  14.9 0.1 broadcast_subtract_fusion
  15.0 16.5 %all-gather.5.cloned.1.call-done = bf16[4096,1024]{1,0:T(8,128)(2,1)} async-done(((bf16[2048,1024]{1,0:T(8,128)(2,1)}), bf16[4096,1024]{1,0:T(8,128)(2,1)}) %all-gather.5.cloned.1.call-update) | async-done | bytes 8388624 | tf_op jit(solution)/shard_map/all_gather | solution.py:44
  31.5 238.5 %all-gather.3.cloned.1.call-done = bf16[2048,4096]{1,0:T(8,128)(2,1)} async-done(((bf16[2048,256]{1,0:T(8,128)(2,1)}), bf16[2048,4096]{1,0:T(8,128)(2,1)}) %all-gather.3.cloned.1.call-update) | async-done | bytes 16777232 | tf_op jit(solution)/shard_map/all_gather | solution.py:46
  270.0 0.0 copy-start
  270.0 24.3 %fusion.20 = f32[2048,1024]{0,1:T(8,128)} fusion(bf16[2048,4096]{1,0:T(8,128)(2,1)} %all-gather.3.cloned.1.call-done, bf16[4096,1024]{1,0:T(8,128)(2,1)} %all-gather.5.cloned.1.call-done), kind=kOutput, calls=%fused_computation.32 | convolution fusion | flops 17179869184 | bytes 33554432 | tf_op jit(solution)/shard_map/dot_general | solution.py:45
  294.3 0.0 copy-done
  294.3 12.7 %convolution_bitcast_fusion = f32[16,2,32,2,32]{2,4,1,3,0:T(8,128)S(1)} fusion(f32[2048,16,2,32,1]{0,3,4,2,1:T(8,128)} %bitcast.33, bf16[2048,16,2,32,1]{0,3,2,4,1:T(8,128)(2,1)S(1)} %bitcast.32), kind=kOutput, calls=%fused_computation | convolution fusion | flops 1610612736 | bytes 12845056 | tf_op jit(solution)/shard_map/gnpi,gnqj->npiqj/dot_general | solution.py:27
  307.0 0.1 fusion.3
  307.1 0.2 copy.21
  307.3 0.2 copy.20
  307.4 0.4 fusion.4
  307.9 0.4 fusion.5
  308.3 0.4 fusion
  308.7 0.4 fusion.1
  309.1 0.7 maximum_multiply_fusion
  309.9 0.0 all-reduce.2.cloned.1.call-update
  309.9 124.9 %all-reduce.2.cloned.1.call-done = f32[2,8,32,32]{3,1,2,0:T(8,128)} async-done(((f32[2,8,32,32]{3,1,2,0:T(8,128)}), f32[2,8,32,32]{3,1,2,0:T(8,128)}) %all-reduce.2.cloned.1.call-update) | async-done | bytes 65552 | tf_op jit(solution)/shard_map/psum | solution.py:55
  434.8 1.7 copy.24
  (2 shorter events, 0.0 us)
Async XLA Ops:
  6.5 8.1 %copy-start.1 = (f32[256]{0:T(256)S(1)}, f32[256]{0:T(256)}, u32[]{:S(2)}) copy-start(f32[256]{0:T(256)} %param.8) | copy-start | bytes 3076
  6.5 8.1 %copy-start.2 = (s32[256]{0:T(256)S(1)}, s32[256]{0:T(256)}, u32[]{:S(2)}) copy-start(s32[256]{0:T(256)} %param.11) | copy-start | bytes 3076
  6.5 8.2 %copy-start.3 = (s32[32]{0:T(128)S(1)}, s32[32]{0:T(128)}, u32[]{:S(2)}) copy-start(s32[32]{0:T(128)} %param.10) | copy-start | bytes 388
  6.5 8.4 %copy-start.4 = (f32[8]{0:T(128)S(1)}, f32[8]{0:T(128)}, u32[]{:S(2)}) copy-start(f32[8]{0:T(128)} %param.9) | copy-start | bytes 100
  6.5 25.0 %all-gather.5.cloned.1.call-start = ((), (), s32[]{:S(2)}) async-start(), calls=%async_computation.1 | async-start | bytes 12582912 | tf_op jit(solution)/shard_map/all_gather | solution.py:44
  7.3 262.8 %all-gather.3.cloned.1.call-start = ((), (), s32[]{:S(2)}) async-start(), calls=%async_computation | async-start | bytes 17825792 | tf_op jit(solution)/shard_map/all_gather | solution.py:46
  8.0 426.8 %all-reduce.2.cloned.1.call-start = ((), (), s32[]{:S(2)}) async-start(), calls=%async_computation.2 | async-start | bytes 524288 | tf_op jit(solution)/shard_map/psum | solution.py:55
  270.0 24.3 %copy-start = (bf16[2048,1024]{0,1:T(8,128)(2,1)S(1)}, bf16[2048,1024]{0,1:T(8,128)(2,1)}, u32[]{:S(2)}) copy-start(bf16[2048,1024]{0,1:T(8,128)(2,1)} %copy.19) | copy-start | bytes 12582916
Sparse Core Ops, SparseCore 0:
  8.9 22.5 all-gather.4
  34.2 235.7 all-gather.2
  310.0 124.7 all-reduce.1
where the time goes:
time: 443 us
  waiting for transfers between devices  381 us (86%)
  matrix products  38.6 us (9%)
  between operations  13.2 us (3%)
  local copies, waits for them, and re-layouts  8.72 us (2%)
    all_gather x1, waiting for transfers between devices, shards(): lax.all_gather(screening, 'blk', axis=1, tiled=True)  239 us
    psum x1, waiting for transfers between devices, shards(): return lax.psum(partial_value, ('blk', 'ga'))  125 us
    dot_general x1, matrix products, shards(): jnp.dot(lax.all_gather(screening, 'blk', axis=1, tiled=True), gathered, p...  24.3 us
    all_gather x1, waiting for transfers between devices, shards(): gathered = lax.all_gather(pair_elements, 'ga', axis=0, tiled=True)  16.5 us
    dot_general x1, matrix products, window_sigma(): jnp.einsum('gnpi,gnqj->npiqj', local_elems, image_cols, precision=lax.Pre...  12.7 us
  transfers between devices with their start and end apart: 3, of which 3 were waited for; matrix products, arithmetic and copies ran while one was open for 2% of the time, Pallas kernels for 0%

commit v1 on v0

v1 whole, which is shorter than its diff:
```python
import functools

import jax
import jax.numpy as jnp
from jax import lax
from jax.experimental import pallas as pl
from jax.experimental.pallas import tpu as pltpu
from jax.sharding import PartitionSpec as P

MESH = pl.DeviceIdType.MESH
CHUNKS = 8


def sigma_kernel(
    n, ga, bw, m_ref, w_ref, a_ref, mbuf, wbuf, wx, s, lsem,
    wxs, wxr, mxs, mxr, mos, mor, mrs, mrr, wzs, wzr, wys, wyr,
):
    rows, cols = m_ref.shape
    half = rows // 2
    kc = w_ref.shape[1]
    nz = n // 4
    cr = rows // CHUNKS
    b, g = lax.axis_index("blk"), lax.axis_index("ga")
    x, y, z = b % 2, (b // 2) % 2, b // 4
    px = b + 1 - 2 * x
    py = b + 2 - 4 * y

    def remote(src, dst, ss, rs, dev):
        return pltpu.make_async_remote_copy(
            src_ref=src, dst_ref=dst, send_sem=ss, recv_sem=rs, device_id=dev, device_id_type=MESH
        )

    def piece(zz, yy, xx):
        return zz * 4 + yy * 2 + xx

    def side(kind):
        return x if kind == 0 else 1 - x

    def w_x():
        return remote(wx, wbuf.at[b], wxs, wxr, (px, g))

    def w_x_in():
        return remote(wx, wbuf.at[px], wxs, wxr, (px, g))

    def w_z(kind, k):
        blk = wbuf.at[piece(z, y, side(kind))]
        return remote(blk, blk, wzs.at[kind, k], wzr.at[kind, k], (piece((z + k) % nz, y, x), g))

    def w_z_in(kind, k):
        blk = wbuf.at[piece((z + nz - k) % nz, y, side(kind))]
        return remote(blk, blk, wzs.at[kind, k], wzr.at[kind, k], (piece((z + k) % nz, y, x), g))

    def w_y(kind, k, row):
        blk = wbuf.at[piece((z + nz - k) % nz, row, side(kind))]
        return remote(blk, blk, wys.at[kind, k], wyr.at[kind, k], (py, g))

    def m_x(c):
        at = pl.ds(pl.multiple_of(g * rows + c * cr, cr), cr)
        return remote(mbuf.at[0, at], mbuf.at[1, at], mxs.at[c], mxr.at[c], (px, g))

    def m_own(k, who):
        blk = mbuf.at[0, pl.ds(pl.multiple_of(who * rows, rows), rows)]
        return remote(blk, blk, mos.at[k], mor.at[k], (b, (g + k) % ga))

    def m_relay(c, k, who):
        blk = mbuf.at[1, pl.ds(pl.multiple_of(who * rows + c * cr, cr), cr)]
        return remote(blk, blk, mrs.at[c, k], mrr.at[c, k], (b, (g + k) % ga))

    def accumulate(h, p):
        step = 512

        @pl.loop(0, cols // step)
        def _(c):
            at = pl.ds(pl.multiple_of(c * step, step), step)
            low = pl.ds(pl.multiple_of(p * kc, kc), kc)
            s[h, :, at] += jnp.dot(wbuf[p], mbuf[h, low, at], preferred_element_type=jnp.float32)

    load_x = pltpu.make_async_copy(w_ref.at[pl.ds(pl.multiple_of((1 - x) * half, half), half)], wx, lsem.at[0])
    load_w = pltpu.make_async_copy(w_ref.at[pl.ds(pl.multiple_of(x * half, half), half)], wbuf.at[b], lsem.at[1])
    load_m = pltpu.make_async_copy(m_ref, mbuf.at[0, pl.ds(pl.multiple_of(g * rows, rows), rows)], lsem.at[2])
    load_x.start()
    load_w.start()
    load_m.start()
    load_x.wait()
    w_x().start()
    load_w.wait()
    w_y(0, 0, y).start()
    for k in range(1, nz):
        w_z(0, k).start()
    load_m.wait()
    for c in range(CHUNKS):
        m_x(c).start()
    for k in range(1, ga):
        m_own(k, g).start()
    s[...] = jnp.zeros_like(s)

    steps = 2 * nz
    done = 0
    for step in range(steps):
        k, kind = step // 2, step % 2
        if step == 1:
            w_x_in().wait_recv()
            for kk in range(1, nz):
                w_z(1, kk).start()
        elif k > 0:
            w_z_in(kind, k).wait_recv()
        if step > 0:
            w_y(kind, k, y).start()
        if step == 0:
            for kk in range(1, ga):
                m_own(kk, (g + ga - kk) % ga).wait_recv()
        accumulate(0, piece((z + nz - k) % nz, y, side(kind)))
        w_y(kind, k, 1 - y).wait_recv()
        while done * steps < (step + 1) * CHUNKS and done < CHUNKS:
            m_x(done).wait_recv()
            for kk in range(1, ga):
                m_relay(done, kk, g).start()
            done += 1
        accumulate(0, piece((z + nz - k) % nz, 1 - y, side(kind)))

    for c in range(CHUNKS):
        for kk in range(1, ga):
            m_relay(c, kk, (g + ga - kk) % ga).wait_recv()

    @pl.loop(0, n)
    def _(p):
        accumulate(1, p)

    mine = pl.ds(pl.multiple_of(g * rows + x * half, half), half)
    wide = 4 * bw
    for h in range(2):

        @pl.loop(0, cols // wide)
        def _(q):
            at = pl.ds(pl.multiple_of(q * wide, wide), wide)
            left = mbuf[h, mine, at]
            image = s[h, :, at]
            high = image.astype(jnp.bfloat16)
            low = (image - high.astype(jnp.float32)).astype(jnp.bfloat16)
            dims = (((0,), (0,)), ((), ()))
            both = lax.dot_general(left, high, dims, preferred_element_type=jnp.float32)
            both += lax.dot_general(left, low, dims, preferred_element_type=jnp.float32)
            for t in range(4):
                a_ref[h, q * 4 + t] = both[t * bw : (t + 1) * bw, t * bw : (t + 1) * bw]

    w_x().wait_send()
    for kind in range(2):
        for k in range(nz):
            w_y(kind, k, y).wait_send()
            if k > 0:
                w_z(kind, k).wait_send()
    for c in range(CHUNKS):
        m_x(c).wait_send()
        for k in range(1, ga):
            m_relay(c, k, g).wait_send()
    for k in range(1, ga):
        m_own(k, g).wait_send()


def intersections(n, ga, bw, elements, screening):
    rows, cols = elements.shape
    half, kc, nz = rows // 2, screening.shape[1], n // 4
    dma = pltpu.SemaphoreType.DMA
    return pl.pallas_call(
        functools.partial(sigma_kernel, n, ga, bw),
        out_shape=jax.ShapeDtypeStruct((2, cols // bw, bw, bw), jnp.float32),
        in_specs=[pl.BlockSpec(memory_space=pl.ANY)] * 2,
        out_specs=pl.BlockSpec(memory_space=pltpu.VMEM),
        scratch_shapes=[
            pltpu.VMEM((2, rows * ga, cols), jnp.bfloat16),
            pltpu.VMEM((n, half, kc), jnp.bfloat16),
            pltpu.VMEM((half, kc), jnp.bfloat16),
            pltpu.VMEM((2, half, cols), jnp.float32),
            dma((3,)),
            dma,
            dma,
            dma((CHUNKS,)),
            dma((CHUNKS,)),
            dma((ga,)),
            dma((ga,)),
            dma((CHUNKS, ga)),
            dma((CHUNKS, ga)),
            dma((2, nz)),
            dma((2, nz)),
            dma((2, nz)),
            dma((2, nz)),
        ],
        compiler_params=pltpu.CompilerParams(has_side_effects=True, vmem_limit_bytes=60 * 2**20),
        name="pair_screen",
    )(elements, screening)


def band_weights(energies, frequencies, qp_index, occupied, offsets, band_count):
    position = jnp.arange(energies.shape[0], dtype=jnp.int32)
    signed = jnp.where(occupied == 1, -energies, energies)
    onehot = (qp_index[:, None] == position[None, :]).astype(jnp.float32)
    state_level = jnp.sum(onehot * signed[None, :], axis=1)
    band_level = jnp.stack([lax.dynamic_slice_in_dim(signed, o, band_count, 0) for o in offsets])
    detuning = state_level[None, None, :] - band_level[:, :, None]
    imag_freq = frequencies[:, None, None, None]
    modulus = detuning[None] ** 2 + imag_freq**2
    return detuning[None] / modulus, -imag_freq / modulus


def shards(n, ga, elements, screening, energies, frequencies, qp_index, occupied):
    states = qp_index.shape[0]
    bands = elements.shape[1] // (2 * states)
    cross = intersections(n, ga, 2 * states, elements, screening)
    real = cross[:, :, :states, :states] + cross[:, :, states:, states:]
    imag = cross[:, :, :states, states:] - cross[:, :, states:, :states]
    b = lax.axis_index("blk")
    offsets = [b * bands, (b + 1 - 2 * (b % 2)) * bands]
    wr, wi = band_weights(energies, frequencies, qp_index, occupied, offsets, bands)
    wr, wi = wr[..., None], wi[..., None]
    sigma_real = jnp.sum(wr * real[None] - wi * imag[None], axis=(1, 2))
    sigma_imag = jnp.sum(wr * imag[None] + wi * real[None], axis=(1, 2))
    total = lax.psum(jnp.stack([sigma_real, sigma_imag]), ("blk", "ga"))
    return total / (elements.shape[0] * ga)


def solution(mesh):
    placed = (P("ga", "blk"), P("ga", "blk"), P(), P(), P(), P())
    body = functools.partial(shards, mesh.shape["blk"], mesh.shape["ga"])
    return jax.shard_map(body, mesh=mesh, in_specs=placed, out_specs=P(), check_vma=False)
```

time: 443 us -> 318 us (0.72)
  waiting for transfers between devices: 381 us -> 147 us
  Pallas kernels: 0 us -> 149 us
  matrix products: 38.6 us -> 0 us
  local copies, waits for them, and re-layouts: 8.72 us -> 0.09 us
  other arithmetic: 1.07 us -> 7.16 us
    all_gather x2 -> x0, waiting for transfers between devices: 255 us -> none  [the longest x1 239 us: shards(): lax.all_gather(screening, 'blk', axis=1, tiled=True)]
    pallas_call x0 -> x1, Pallas kernels: none -> 149 us  [intersections(): pl.pallas_call(functools.partial(sigma_kernel, n, ga, bw), out_shape=jax....]
    dot_general x6 -> x0, matrix products: 38.6 us -> none  [the longest x1 24.3 us: shards(): jnp.dot(lax.all_gather(screening, 'blk', axis=1, tiled=True), gathered, p...]
    psum x1, waiting for transfers between devices: 125 us -> 147 us  [shards(): total = lax.psum(jnp.stack([sigma_real, sigma_imag]), ('blk', 'ga'))]
    unnamed x11 -> x8, local copies, waits for them, and re-layouts: 6.61 us -> 0.01 us
  transfers between devices with their start and end apart: 3 -> 1, of which waited for: 3 -> 1; matrix products, arithmetic and copies ran while one was open for 2% -> 0% of each run, Pallas kernels for 0% -> 0%
where the time goes in v1:
time: 318 us; the launch traced here: 317 us
  Pallas kernels  149 us (47%)
  waiting for transfers between devices  147 us (46%)
  between operations  13.5 us (4%)
  other arithmetic  7.16 us (2%)
    pallas_call x1, Pallas kernels, intersections(): pl.pallas_call(functools.partial(sigma_kernel, n, ga, bw), out_shape=jax....  149 us
    psum x1, waiting for transfers between devices, shards(): total = lax.psum(jnp.stack([sigma_real, sigma_imag]), ('blk', 'ga'))  147 us
  transfers between devices with their start and end apart: 1, of which 1 were waited for; matrix products, arithmetic and copies ran while one was open for 0% of the time, Pallas kernels for 0%

profile of v1, /device:TPU:0, one launch (start us, length us, event | category | flops | bytes accessed | tf_op | source)
XLA Modules:
  0.0 317.4 jit_solution(6860437150895486504)
XLA Ops:
  6.5 0.0 all-reduce.2.cloned.1.call-start
  6.5 0.0 copy-start.3
  6.5 0.0 copy-start
  6.5 0.0 copy-start.1
  6.5 0.0 copy-start.2
  6.5 149.2 %pair_screen.1 = f32[2,16,64,64]{3,2,1,0:T(8,128)} custom-call(bf16[2048,1024]{1,0:T(8,128)(2,1)} %m_ref.1, bf16[2048,256]{1,0:T(8,128)(2,1)} %w_ref.1), custom_call_target="tpu_custom_call" | custom-call | tf_op jit(solution)/shard_map/pair_screen/pallas_call | solution.py:164
  155.8 1.9 slice_add_fusion
  157.6 0.0 copy-done.3
  157.7 0.0 copy-done
  157.7 0.0 copy-done.1
  157.7 0.0 copy-done.2
  157.7 0.2 select_reduce_fusion
  157.9 0.1 dynamic-slice_bitcast_fusion.1
  158.0 0.1 broadcast_subtract_fusion
  158.0 0.1 add_divide_fusion.1
  158.2 2.5 subtract_reduce_fusion
  160.7 0.7 pad_maximum_fusion
  161.4 0.0 all-reduce.2.cloned.1.call-update
  161.4 147.5 %all-reduce.2.cloned.1.call-done = f32[2,8,32,32]{3,2,1,0:T(8,128)} async-done(((f32[2,8,32,32]{3,2,1,0:T(8,128)}), f32[2,8,32,32]{3,2,1,0:T(8,128)}) %all-reduce.2.cloned.1.call-update) | async-done | bytes 65552 | tf_op jit(solution)/shard_map/psum | solution.py:217
  308.9 1.7 broadcast_multiply_fusion
  (3 shorter events, 0.0 us)
Async XLA Ops:
  6.5 302.4 %all-reduce.2.cloned.1.call-start = ((), (), s32[]{:S(2)}) async-start(), calls=%async_computation | async-start | bytes 524288 | tf_op jit(solution)/shard_map/psum | solution.py:217
  6.5 151.1 %copy-start.3 = (f32[8]{0:T(128)S(1)}, f32[8]{0:T(128)}, u32[]{:S(2)}) copy-start(f32[8]{0:T(128)} %param.9) | copy-start | bytes 100
  6.5 151.1 %copy-start = (f32[256]{0:T(256)S(1)}, f32[256]{0:T(256)}, u32[]{:S(2)}) copy-start(f32[256]{0:T(256)} %param.8) | copy-start | bytes 3076
  6.5 151.1 %copy-start.1 = (s32[256]{0:T(256)S(1)}, s32[256]{0:T(256)}, u32[]{:S(2)}) copy-start(s32[256]{0:T(256)} %param.11) | copy-start | bytes 3076
  6.5 151.2 %copy-start.2 = (s32[32]{0:T(128)S(1)}, s32[32]{0:T(128)}, u32[]{:S(2)}) copy-start(s32[32]{0:T(128)} %param.10) | copy-start | bytes 388
Sparse Core Ops, SparseCore 0:
  161.5 147.3 all-reduce.1

commit v2 on v1

--- a/solution.py
+++ b/solution.py
@@ -8,7 +8,6 @@
 from jax.sharding import PartitionSpec as P
 
 MESH = pl.DeviceIdType.MESH
-CHUNKS = 8
 
 
 def sigma_kernel(
@@ -19,7 +18,9 @@
     half = rows // 2
     kc = w_ref.shape[1]
     nz = n // 4
-    cr = rows // CHUNKS
+    layers = nz // ga
+    chunks = 4 * layers
+    cr = rows // chunks
     b, g = lax.axis_index("blk"), lax.axis_index("ga")
     x, y, z = b % 2, (b // 2) % 2, b // 4
     px = b + 1 - 2 * x
@@ -54,8 +55,15 @@
         blk = wbuf.at[piece((z + nz - k) % nz, row, side(kind))]
         return remote(blk, blk, wys.at[kind, k], wyr.at[kind, k], (py, g))
 
+    def layer(who, u):
+        start = jnp.where(z // layers == who, z % layers, layers - 1)
+        return who * layers + (start + layers - u) % layers
+
+    def m_rows(who, c):
+        return pl.ds(pl.multiple_of((layer(who, c // 4) * 4 + c % 4) * cr, cr), cr)
+
     def m_x(c):
-        at = pl.ds(pl.multiple_of(g * rows + c * cr, cr), cr)
+        at = m_rows(g, c)
         return remote(mbuf.at[0, at], mbuf.at[1, at], mxs.at[c], mxr.at[c], (px, g))
 
     def m_own(k, who):
@@ -63,7 +71,7 @@
         return remote(blk, blk, mos.at[k], mor.at[k], (b, (g + k) % ga))
 
     def m_relay(c, k, who):
-        blk = mbuf.at[1, pl.ds(pl.multiple_of(who * rows + c * cr, cr), cr)]
+        blk = mbuf.at[1, m_rows(who, c)]
         return remote(blk, blk, mrs.at[c, k], mrr.at[c, k], (b, (g + k) % ga))
 
     def accumulate(h, p):
@@ -74,6 +82,28 @@
             at = pl.ds(pl.multiple_of(c * step, step), step)
             low = pl.ds(pl.multiple_of(p * kc, kc), kc)
             s[h, :, at] += jnp.dot(wbuf[p], mbuf[h, low, at], preferred_element_type=jnp.float32)
+
+    def accumulate_layer(zz):
+        step = 512
+
+        @pl.loop(0, cols // step)
+        def _(c):
+            at = pl.ds(pl.multiple_of(c * step, step), step)
+            total = s[1, :, at]
+            for t in range(4):
+                low = pl.ds(pl.multiple_of((zz * 4 + t) * kc, kc), kc)
+                total += jnp.dot(wbuf[zz * 4 + t], mbuf[1, low, at], preferred_element_type=jnp.float32)
+            s[1, :, at] = total
+
+    def early():
+        for c in range(4):
+            for kk in range(1, ga):
+                m_relay(c, kk, (g + ga - kk) % ga).wait_recv()
+
+    def first(who, zz):
+        return who * layers + (zz % layers if zz // layers == who else layers - 1)
+
+    reach = max((zz - first(who, zz)) % nz for zz in range(nz) for who in range(ga))
 
     load_x = pltpu.make_async_copy(w_ref.at[pl.ds(pl.multiple_of((1 - x) * half, half), half)], wx, lsem.at[0])
     load_w = pltpu.make_async_copy(w_ref.at[pl.ds(pl.multiple_of(x * half, half), half)], wbuf.at[b], lsem.at[1])
@@ -88,7 +118,7 @@
     for k in range(1, nz):
         w_z(0, k).start()
     load_m.wait()
-    for c in range(CHUNKS):
+    for c in range(chunks):
         m_x(c).start()
     for k in range(1, ga):
         m_own(k, g).start()
@@ -96,6 +126,7 @@
 
     steps = 2 * nz
     done = 0
+    swept = 0
     for step in range(steps):
         k, kind = step // 2, step % 2
         if step == 1:
@@ -111,20 +142,30 @@
                 m_own(kk, (g + ga - kk) % ga).wait_recv()
         accumulate(0, piece((z + nz - k) % nz, y, side(kind)))
         w_y(kind, k, 1 - y).wait_recv()
-        while done * steps < (step + 1) * CHUNKS and done < CHUNKS:
+        while done * steps < (step + 1) * chunks and done < chunks:
             m_x(done).wait_recv()
             for kk in range(1, ga):
                 m_relay(done, kk, g).start()
             done += 1
         accumulate(0, piece((z + nz - k) % nz, 1 - y, side(kind)))
-
-    for c in range(CHUNKS):
+        if step == 2 * reach + 2:
+            early()
+        if step >= 2 * reach + 2 and done >= 4:
+            while swept < ga and swept * (steps - 2 * reach - 2) < (step - 2 * reach - 1) * ga:
+                accumulate_layer(layer(swept, 0))
+                swept += 1
+
+    if 2 * reach + 2 >= steps:
+        early()
+    for c in range(4, chunks):
         for kk in range(1, ga):
             m_relay(c, kk, (g + ga - kk) % ga).wait_recv()
 
-    @pl.loop(0, n)
-    def _(p):
-        accumulate(1, p)
+    for who in range(swept, ga):
+        accumulate_layer(layer(who, 0))
+    for who in range(ga):
+        for u in range(1, layers):
+            accumulate_layer(layer(who, u))
 
     mine = pl.ds(pl.multiple_of(g * rows + x * half, half), half)
     wide = 4 * bw
@@ -149,7 +190,7 @@
             w_y(kind, k, y).wait_send()
             if k > 0:
                 w_z(kind, k).wait_send()
-    for c in range(CHUNKS):
+    for c in range(chunks):
         m_x(c).wait_send()
         for k in range(1, ga):
             m_relay(c, k, g).wait_send()
@@ -160,6 +201,7 @@
 def intersections(n, ga, bw, elements, screening):
     rows, cols = elements.shape
     half, kc, nz = rows // 2, screening.shape[1], n // 4
+    chunks = 4 * (nz // ga)
     dma = pltpu.SemaphoreType.DMA
     return pl.pallas_call(
         functools.partial(sigma_kernel, n, ga, bw),
@@ -174,12 +216,12 @@
             dma((3,)),
             dma,
             dma,
-            dma((CHUNKS,)),
-            dma((CHUNKS,)),
+            dma((chunks,)),
+            dma((chunks,)),
             dma((ga,)),
             dma((ga,)),
-            dma((CHUNKS, ga)),
-            dma((CHUNKS, ga)),
+            dma((chunks, ga)),
+            dma((chunks, ga)),
             dma((2, nz)),
             dma((2, nz)),
             dma((2, nz)),
@@ -188,6 +230,48 @@
         compiler_params=pltpu.CompilerParams(has_side_effects=True, vmem_limit_bytes=60 * 2**20),
         name="pair_screen",
     )(elements, screening)
+
+
+def sum_kernel(n, ga, part_ref, out_ref, inbox, sem):
+    count = n * ga
+    me = lax.axis_index("blk") * ga + lax.axis_index("ga")
+
+    def remote(src, dst, phase, k):
+        to = (me + k) % count
+        return pltpu.make_async_remote_copy(
+            src_ref=src, dst_ref=dst, send_sem=sem.at[phase, 0], recv_sem=sem.at[phase, 1],
+            device_id=(to // ga, to % ga), device_id_type=MESH,
+        )
+
+    @pl.loop(1, count)
+    def _(k):
+        remote(part_ref.at[(me + k) % count], inbox.at[k - 1], 0, k).start()
+
+    remote(inbox, inbox, 0, 1).wait_recv()
+    out_ref[me] = part_ref[me] + jnp.sum(inbox[...], axis=0)
+
+    @pl.loop(1, count)
+    def _(k):
+        remote(out_ref.at[me], out_ref.at[me], 1, k).start()
+
+    remote(inbox, inbox, 0, 1).wait_send()
+    remote(inbox, inbox, 1, 1).wait_recv()
+    remote(inbox, inbox, 1, 1).wait_send()
+
+
+def sum_everywhere(n, ga, part):
+    count = n * ga
+    width = part.size // count
+    vmem = pl.BlockSpec(memory_space=pltpu.VMEM)
+    return pl.pallas_call(
+        functools.partial(sum_kernel, n, ga),
+        out_shape=jax.ShapeDtypeStruct((count, 1, width), jnp.float32),
+        in_specs=[vmem],
+        out_specs=vmem,
+        scratch_shapes=[pltpu.VMEM((count - 1, 1, width), jnp.float32), pltpu.SemaphoreType.DMA((2, 2))],
+        compiler_params=pltpu.CompilerParams(has_side_effects=True),
+        name="sum_all",
+    )(part.reshape(count, 1, width)).reshape(part.shape)
 
 
 def band_weights(energies, frequencies, qp_index, occupied, offsets, band_count):
@@ -214,8 +298,8 @@
     wr, wi = wr[..., None], wi[..., None]
     sigma_real = jnp.sum(wr * real[None] - wi * imag[None], axis=(1, 2))
     sigma_imag = jnp.sum(wr * imag[None] + wi * real[None], axis=(1, 2))
-    total = lax.psum(jnp.stack([sigma_real, sigma_imag]), ("blk", "ga"))
-    return total / (elements.shape[0] * ga)
+    share = jnp.stack([sigma_real, sigma_imag]) / (elements.shape[0] * ga)
+    return sum_everywhere(n, ga, share)
 
 
 def solution(mesh):

time: 318 us -> 189 us (0.59)
  waiting for transfers between devices: 147 us -> 0 us
  Pallas kernels: 149 us -> 181 us
  between operations: 13.5 us -> 0.11 us
    psum x1 -> x0, waiting for transfers between devices: 147 us -> none  [shards(): total = lax.psum(jnp.stack([sigma_real, sigma_imag]), ('blk', 'ga'))]
    pallas_call x0 -> x1, Pallas kernels: none -> 36 us  [sum_everywhere(): pl.pallas_call(functools.partial(sum_kernel, n, ga), out_shape=jax.ShapeD...]
    pallas_call x1, Pallas kernels: 149 us -> 145 us  [intersections(): pl.pallas_call(functools.partial(sigma_kernel, n, ga, bw), out_shape=jax....]
  transfers between devices with their start and end apart: 1 -> 0, of which waited for: 1 -> 0; matrix products, arithmetic and copies ran while one was open for 0% -> 0% of each run, Pallas kernels for 0% -> 0%
where the time goes in v2:
time: 189 us
  Pallas kernels  181 us (96%)
  other arithmetic  5.79 us (3%)
    pallas_call x1, Pallas kernels, intersections(): pl.pallas_call(functools.partial(sigma_kernel, n, ga, bw), out_shape=jax....  145 us
    pallas_call x1, Pallas kernels, sum_everywhere(): pl.pallas_call(functools.partial(sum_kernel, n, ga), out_shape=jax.ShapeD...  36 us

profile of v2, /device:TPU:0, one launch (start us, length us, event | category | flops | bytes accessed | tf_op | source)
XLA Modules:
  0.0 188.8 jit_solution(15672398431468166801)
XLA Ops:
  0.0 0.0 copy-start.3
  0.0 0.0 copy-start
  0.0 0.0 copy-start.1
  0.0 0.0 copy-start.2
  0.0 145.2 %pair_screen.1 = f32[2,16,64,64]{3,2,1,0:T(8,128)} custom-call(bf16[2048,1024]{1,0:T(8,128)(2,1)} %m_ref.1, bf16[2048,256]{1,0:T(8,128)(2,1)} %w_ref.1), custom_call_target="tpu_custom_call" | custom-call | tf_op jit(solution)/shard_map/pair_screen/pallas_call | solution.py:206
  145.3 1.9 slice_add_fusion
  147.1 0.0 copy-done.3
  147.2 0.0 copy-done
  147.2 0.0 copy-done.1
  147.2 0.1 dynamic-slice_bitcast_fusion.1
  147.3 0.0 copy-done.2
  147.3 0.2 select_reduce_fusion
  147.5 0.1 broadcast_subtract_fusion
  147.6 0.1 add_divide_fusion.1
  147.7 2.5 %subtract_reduce_fusion = (f32[8,32,32]{2,1,0:T(8,128)S(1)}, f32[8,32,32]{2,1,0:T(8,128)S(1)}) fusion(f32[2,16,32,32]{3,2,1,0:T(8,128)S(1)} %get-tuple-element.8, f32[8,2,16,32]{3,2,1,0:T(8,128)S(1)} %get-tuple-element.10, f32[2,16,32,32]{3,2,1,0:T(8,128)S(1)} %get-tuple-element.7, f32[8,2,16,32]{3,2,1,0:T(8,128)S(1)} %get-tuple-element.9), kind=kLoop, calls=%fused_computation.1 | loop fusion | flops 2080768 | bytes 393216 | tf_op jit(solution)/shard_map/reduce_sum | solution.py:299
  150.2 0.8 div.38.part_ref
  151.0 36.0 %sum_all.1 = f32[32,1,512]{2,1,0:T(1,128)} custom-call(f32[32,1,512]{2,1,0:T(1,128)} %div.38.part_ref), custom_call_target="tpu_custom_call" | custom-call | tf_op jit(solution)/shard_map/sum_all/pallas_call | solution.py:266
  187.0 1.0 reduce
  188.0 0.8 reshape.32
  (4 shorter events, 0.0 us)
Async XLA Ops:
  0.0 147.1 %copy-start.3 = (f32[8]{0:T(128)S(1)}, f32[8]{0:T(128)}, u32[]{:S(2)}) copy-start(f32[8]{0:T(128)} %param.9) | copy-start | bytes 100
  0.0 147.2 %copy-start = (f32[256]{0:T(256)S(1)}, f32[256]{0:T(256)}, u32[]{:S(2)}) copy-start(f32[256]{0:T(256)} %param.8) | copy-start | bytes 3076
  0.0 147.2 %copy-start.1 = (s32[256]{0:T(256)S(1)}, s32[256]{0:T(256)}, u32[]{:S(2)}) copy-start(s32[256]{0:T(256)} %param.11) | copy-start | bytes 3076
  0.0 147.3 %copy-start.2 = (s32[32]{0:T(128)S(1)}, s32[32]{0:T(128)}, u32[]{:S(2)}) copy-start(s32[32]{0:T(128)} %param.10) | copy-start | bytes 388
